TPU v7x, 32 devices: a whole 2x2x4 slice. The times are simulated.
32 devices in a mesh: blk: 8 (over z, y), batch: 4 (over x, core).
Axes of the slice: x: 2, y: 2, z: 4, core: 2. Of those that a mesh axis runs over, the one named last changes fastest.
Arguments:
- coefficients: bfloat16 [120, 24576], P(None, ('blk', 'batch')), may hold values from -6 to 6
- transforms: bfloat16 [12, 24, 24576], P(None, 'batch', 'blk'), may hold values from -6 to 6
- basis: bfloat16 [120, 3, 4096], P(None, None, 'blk'), may hold values from -0.5 to 0.5
- template: bfloat16 [3, 4096], P(None, 'blk'), may hold values from -6 to 6
- skin_weights: bfloat16 [24, 4096], P(None, 'blk'), may hold values from 0.019897461 to 1
Outputs:
- skinned: bfloat16 [24576, 4, 3, 512], P(('blk', 'batch'))
All inputs are finite; a program needn't handle non-finite values.
Results may differ from a plain program's by a relative error of at most 0.0049.
Values may be sent and summed in bfloat16 or wider, within the bound.
A program may use at most 192 MiB of HBM per device.

v0:
```python
import jax
import jax.numpy as jnp
from jax import lax
from jax.sharding import PartitionSpec as P

STEPS = 4


def as_sent(x):
    return jax.tree.map(lambda a: a.astype(jnp.bfloat16) if a.dtype == jnp.float32 else a, x)


def passed_along(block, axis, distance):
    devices = range(lax.axis_size(axis))
    route = [((i - distance) % len(devices), i) for i in devices]
    return lax.ppermute(block, axis, route)


def skin_block(coefficients, joint_poses, basis_block, template_block, weight_block):
    flattened = basis_block.reshape(basis_block.shape[0], -1)
    shaped = lax.dot_general(
        coefficients, flattened, (((0,), (0,)), ((), ())), preferred_element_type=jnp.float32
    )
    shaped = shaped + template_block.reshape(1, -1).astype(jnp.float32)
    shaped = shaped.reshape(coefficients.shape[1], 3, -1)
    blended = jnp.einsum(
        "mjr,jv->mrv", joint_poses, weight_block, preferred_element_type=jnp.float32
    )
    positions = []
    for matrix_row in range(3):
        component = blended[4 * matrix_row + 3]
        for column in range(3):
            component = component + blended[4 * matrix_row + column] * shaped[:, column, :]
        positions.append(component)
    return jnp.stack(positions, axis=1).astype(jnp.bfloat16)


def normalize(skin_weights):
    weight_float = skin_weights.astype(jnp.float32)
    return (weight_float / jnp.sum(weight_float, axis=0, keepdims=True)).astype(jnp.bfloat16)


def per_device(coefficients, transforms, basis, template, skin_weights):
    normalized = normalize(skin_weights)
    joint_poses = lax.all_to_all(transforms, "batch", split_axis=2, concat_axis=1, tiled=True)
    resident = (basis, template, normalized)
    stacked = tuple((member[None] for member in resident))
    covered = 1
    while covered < STEPS:
        shifted = jax.tree.map(
            lambda part, own: part.astype(own.dtype),
            passed_along(as_sent(stacked), "blk", covered),
            stacked,
        )
        stacked = tuple(
            (
                jnp.concatenate([current, arrived], axis=0)
                for current, arrived in zip(stacked, shifted)
            )
        )
        covered = covered * 2
    sources = [tuple((member[slot_index] for member in stacked)) for slot_index in range(STEPS)]
    outputs = [
        skin_block(coefficients, joint_poses, source[0], source[1], source[2]) for source in sources
    ]
    return jnp.stack(outputs, axis=1)


def solution(mesh):
    in_specs = (
        P(None, ("blk", "batch")),
        P(None, "batch", "blk"),
        P(None, None, "blk"),
        P(None, "blk"),
        P(None, "blk"),
    )
    out_specs = P(("blk", "batch"), None, None, None)
    return jax.shard_map(
        per_device, mesh=mesh, in_specs=in_specs, out_specs=out_specs, check_vma=False
    )
```

profile of v0, /device:TPU:0, one launch (start us, length us, event | category | flops | bytes accessed | tf_op | source)
XLA Modules:
  0.0 153.3 jit_solution(1806973865037193045)
XLA Ops:
  0.0 3.0 %collective-permute-start.2 = (bf16[1,3,512]{2,1,0:T(4,128)(2,1)}, bf16[1,3,512]{2,1,0:T(4,128)(2,1)S(1)}, u32[]{:S(2)}, u32[]{:S(2)}) collective-permute-start(bf16[1,3,512]{2,1,0:T(4,128)(2,1)} %bitcast.532), channel_id=1, source_target_pairs={{28,0},{0,4},{4,8},{8,12},{12,16},{16,20},{20,24},{24,28},{29,1},{... | collective-permute-start | bytes 9224 | tf_op jit(solution)/shard_map/ppermute | solution.py:16
  3.0 0.8 convert_reduce_fusion
  3.8 0.7 fusion.99
  4.5 1.6 %collective-permute-start = (bf16[1,24,512]{2,1,0:T(8,128)(2,1)S(1)}, bf16[1,24,512]{2,1,0:T(8,128)(2,1)S(1)}, u32[]{:S(2)}, u32[]{:S(2)}) collective-permute-start(bf16[1,24,512]{2,1,0:T(8,128)(2,1)S(1)} %fusion.99), channel_id=1, source_target_pairs={{28,0},{0,4},{4,8},{8,12},{12,16},{16,20},{20,24},{24,28},{29,1},{... | collective-permute-start | bytes 73736 | tf_op jit(solution)/shard_map/ppermute | solution.py:16
  6.1 6.5 %copy.27 = bf16[12,6,3072]{0,1,2:T(8,128)(2,1)} copy(bf16[12,6,3072]{2,1,0:T(8,128)(2,1)} %param.6) | data formatting | bytes 884736 | tf_op args[1]
  12.6 8.0 %reshape.289 = bf16[4,2,27648]{2,1,0:T(2,128)(2,1)} reshape(bf16[3072,6,12]{2,1,0:T(8,128)(2,1)} %bitcast.524) | data formatting | bytes 884736
  20.6 3.6 %all-to-all-start = ((bf16[4,2,27648]{2,1,0:T(2,128)(2,1)}), bf16[4,2,27648]{2,1,0:T(2,128)(2,1)S(1)}, u32[]{:S(2)}, u32[]{:S(2)}) async-start(bf16[4,2,27648]{2,1,0:T(2,128)(2,1)} %reshape.289), calls=%async_computation | async-start | bytes 884736 | tf_op jit(solution)/shard_map/all_to_all | solution.py:45
  24.2 1.6 %collective-permute-start.1 = (bf16[1,120,3,512]{3,1,2,0:T(8,128)(2,1)S(1)}, bf16[1,120,3,512]{3,1,2,0:T(8,128)(2,1)S(1)}, u32[]{:S(2)}, u32[]{:S(2)}) collective-permute-start(bf16[1,120,3,512]{3,1,2,0:T(8,128)(2,1)S(1)} %bitcast.530), channel_id=1, source_target_pairs={{28,0},{0,4},{4,8},{8,12},{12,16},{16,20},{20,24},{24,28},{29,1},{... | collective-permute-start | bytes 1105928 | tf_op jit(solution)/shard_map/ppermute | solution.py:16
  25.8 0.2 copy.29
  26.0 0.0 collective-permute-done.2
  26.0 1.6 %collective-permute-start.5 = (bf16[2,3,512]{2,1,0:T(4,128)(2,1)S(1)}, bf16[2,3,512]{2,1,0:T(4,128)(2,1)S(1)}, u32[]{:S(2)}, u32[]{:S(2)}) collective-permute-start(bf16[2,3,512]{2,1,0:T(4,128)(2,1)S(1)} %pad_maximum_fusion.2), channel_id=1, source_target_pairs={{24,0},{28,4},{0,8},{4,12},{8,16},{12,20},{16,24},{20,28},{25,1},{... | collective-permute-start | bytes 18440 | tf_op jit(solution)/shard_map/ppermute | solution.py:16
  27.7 3.0 %convolution_add_fusion.3 = f32[768,1536]{1,0:T(8,128)} fusion(bf16[120,768]{1,0:T(8,128)(2,1)S(1)} %copy-done, bf16[120,1536]{0,1:T(8,128)(2,1)S(1)} %bitcast.526, f32[1536]{0:T(1024)S(1)} %reshape.281), kind=kOutput, calls=%fused_computation.8 | convolution fusion | flops 284295168 | bytes 5277696 | tf_op jit(solution)/shard_map/dot_general | solution.py:21
  30.7 6.0 %copy.30 = f32[768,1536]{0,1:T(8,128)} copy(f32[768,1536]{1,0:T(8,128)} %convolution_add_fusion.3) | data formatting | bytes 9437184 | tf_op jit(solution)/shard_map/add | solution.py:24
  36.8 0.0 collective-permute-done
  36.8 1.8 %collective-permute-start.3 = (bf16[2,24,512]{2,1,0:T(8,128)(2,1)S(1)}, bf16[2,24,512]{2,1,0:T(8,128)(2,1)S(1)}, u32[]{:S(2)}, u32[]{:S(2)}) collective-permute-start(bf16[2,24,512]{2,1,0:T(8,128)(2,1)S(1)} %pad_maximum_fusion.1), channel_id=1, source_target_pairs={{24,0},{28,4},{0,8},{4,12},{8,16},{12,20},{16,24},{20,28},{25,1},{... | collective-permute-start | bytes 147464 | tf_op jit(solution)/shard_map/ppermute | solution.py:16
  38.6 7.5 %reshape.290 = bf16[3072,6,12]{2,1,0:T(8,128)(2,1)} reshape(bf16[4,2,27648]{2,1,0:T(2,128)(2,1)S(1)} %all-to-all-done) | data formatting | bytes 884736
  46.1 6.7 %copy.28 = bf16[12,6,4,768]{3,1,2,0:T(8,128)(2,1)S(1)} copy(bf16[12,6,4,768]{0,1,3,2:T(8,128)(2,1)} %bitcast.523) | data formatting | bytes 884736 | tf_op jit(solution)/shard_map/all_to_all | solution.py:45
  52.8 0.1 all_to_all.16
  53.0 2.7 %convolution_bitcast_fusion.3 = f32[12,768,512]{1,2,0:T(8,128)S(1)} fusion(bf16[12,24,768]{2,1,0:T(8,128)(2,1)S(1)} %all_to_all.16, bf16[24,512]{1,0:T(8,128)(2,1)S(1)} %copy-done.10, f32[512]{0:T(512)S(1)} %convert_reduce_fusion), kind=kOutput, calls=%fused_computation.4 | convolution fusion | flops 226529280 | bytes 19343360 | tf_op jit(solution)/shard_map/mjr,jv->mrv/dot_general | solution.py:26
  55.7 8.1 %convolution_bitcast_fusion = f32[12,768,512]{1,2,0:T(8,128)} fusion(bf16[12,24,768]{2,1,0:T(8,128)(2,1)S(1)} %all_to_all.16, bf16[2,24,512]{2,1,0:T(8,128)(2,1)S(1)} %collective-permute-done.3), kind=kOutput, calls=%fused_computation.1 | convolution fusion | flops 226492416 | bytes 19341312 | tf_op jit(solution)/shard_map/mjr,jv->mrv/dot_general | solution.py:26
  63.8 8.1 %convolution_bitcast_fusion.1 = f32[12,768,512]{1,2,0:T(8,128)} fusion(bf16[12,24,768]{2,1,0:T(8,128)(2,1)S(1)} %all_to_all.16, bf16[2,24,512]{2,1,0:T(8,128)(2,1)S(1)} %collective-permute-done.3), kind=kOutput, calls=%fused_computation.2 | convolution fusion | flops 226492416 | bytes 19341312 | tf_op jit(solution)/shard_map/mjr,jv->mrv/dot_general | solution.py:26
  71.8 8.0 %convolution_bitcast_fusion.2 = f32[12,768,512]{1,2,0:T(8,128)} fusion(bf16[12,24,768]{2,1,0:T(8,128)(2,1)S(1)} %all_to_all.16, bf16[1,24,512]{2,1,0:T(8,128)(2,1)S(1)} %collective-permute-done), kind=kOutput, calls=%fused_computation.3 | convolution fusion | flops 226492416 | bytes 19341312 | tf_op jit(solution)/shard_map/mjr,jv->mrv/dot_general | solution.py:26
  79.9 1.1 fusion.84
  81.0 1.5 fusion.86
  82.5 1.0 pad_maximum_fusion
  83.5 0.2 collective-permute-start.4
  83.7 0.2 copy.31
  83.9 3.0 %convolution_add_fusion.2 = f32[768,1536]{1,0:T(8,128)} fusion(bf16[120,768]{1,0:T(8,128)(2,1)S(1)} %copy-done, bf16[120,1536]{0,1:T(8,128)(2,1)S(1)} %bitcast.529, f32[1536]{0:T(1024)S(1)} %reshape.282), kind=kOutput, calls=%fused_computation.7 | convolution fusion | flops 284295168 | bytes 5277696 | tf_op jit(solution)/shard_map/dot_general | solution.py:21
  86.9 6.0 %copy.32 = f32[768,1536]{0,1:T(8,128)} copy(f32[768,1536]{1,0:T(8,128)} %convolution_add_fusion.2) | data formatting | bytes 9437184 | tf_op jit(solution)/shard_map/add | solution.py:24
  93.0 5.8 %fusion.89 = bf16[768,1,1,512]{0,3,2,1:T(8,128)(2,1)} fusion(f32[768,3,512]{0,2,1:T(8,128)} %bitcast.521, f32[12,768,512]{1,2,0:T(8,128)} %convolution_bitcast_fusion.2), kind=kLoop, calls=%fused_computation.146 | loop fusion | flops 2752512 | bytes 11796480 | tf_op jit(solution)/shard_map/stack | solution.py:35
  98.8 5.3 %fusion.87 = (bf16[768,1,1,512]{0,3,2,1:T(8,128)(2,1)S(1)}, bf16[768,1,1,512]{0,3,2,1:T(8,128)(2,1)S(1)}) fusion(f32[768,3,512]{0,2,1:T(8,128)S(1)} %bitcast.522, f32[12,768,512]{1,2,0:T(8,128)} %convolution_bitcast_fusion.2), kind=kLoop, calls=%fused_computation.144 | loop fusion | flops 5505024 | bytes 18874368 | tf_op jit(solution)/shard_map/stack | solution.py:35
  104.1 2.0 %fusion.101 = (bf16[1,120,3,512]{3,1,2,0:T(8,128)(2,1)}, bf16[1,120,3,512]{3,1,2,0:T(8,128)(2,1)}) fusion(bf16[2,120,3,512]{3,1,2,0:T(8,128)(2,1)} %collective-permute-done.4), kind=kLoop, calls=%fused_computation.166 | loop fusion | bytes 1474560 | tf_op jit(solution)/shard_map/slice | solution.py:62
  106.2 1.9 %copy.33 = bf16[1,120,3,512]{1,3,2,0:T(8,128)(2,1)} copy(bf16[1,120,3,512]{3,1,2,0:T(8,128)(2,1)} %get-tuple-element.13) | data formatting | bytes 737280 | tf_op jit(solution)/shard_map/slice | solution.py:62
  108.1 1.9 %copy.34 = bf16[1,120,3,512]{1,3,2,0:T(8,128)(2,1)} copy(bf16[1,120,3,512]{3,1,2,0:T(8,128)(2,1)} %get-tuple-element.14) | data formatting | bytes 737280 | tf_op jit(solution)/shard_map/slice | solution.py:62
  110.0 1.8 %convolution_add_fusion.1 = f32[1536,768]{1,0:T(8,128)S(1)} fusion(bf16[120,1536]{0,1:T(8,128)(2,1)} %bitcast.527, bf16[120,768]{1,0:T(8,128)(2,1)S(1)} %copy-done, f32[1536]{0:T(1024)S(1)} %reshape.283), kind=kOutput, calls=%fused_computation.6 | convolution fusion | flops 284295168 | bytes 5277696 | tf_op jit(solution)/shard_map/dot_general | solution.py:21
  111.8 0.8 convolution_add_fusion
  112.6 6.6 %fusion.90 = (bf16[768,1,1,512]{0,3,2,1:T(8,128)(2,1)}, bf16[768,1,1,512]{0,3,2,1:T(8,128)(2,1)}) fusion(f32[768,3,512]{0,2,1:T(8,128)S(1)} %bitcast.519, f32[12,768,512]{1,2,0:T(8,128)} %convolution_bitcast_fusion.1), kind=kLoop, calls=%fused_computation.147 | loop fusion | flops 5505024 | bytes 18874368 | tf_op jit(solution)/shard_map/stack | solution.py:35
  119.3 7.3 %fusion.92 = (bf16[768,1,1,512]{0,3,2,1:T(8,128)(2,1)}, bf16[768,1,1,512]{0,3,2,1:T(8,128)(2,1)}) fusion(f32[768,3,512]{0,2,1:T(8,128)S(1)} %bitcast.520, f32[12,768,512]{1,2,0:T(8,128)} %convolution_bitcast_fusion.1, f32[768,3,512]{0,2,1:T(8,128)S(1)} %bitcast.517, f32[12,768,512]{1,2,0:T(8,128)} %convolution_bitcast_fusion), kind=kLoop, calls=%fused_computation.149 | loop fusion | flops 5505024 | bytes 23592960 | tf_op jit(solution)/shard_map/stack | solution.py:35
  126.6 0.2 slice-done.3
  126.9 0.9 slice-done.4
  127.8 1.2 fusion.93
  129.0 0.1 copy-done.3
  129.1 0.2 copy-done.4
  129.4 0.2 copy-done.5
  129.6 0.2 copy-done.6
  129.8 0.2 copy-done.7
  130.1 6.7 %maximum_maximum_fusion = bf16[768,4,3,512]{0,3,2,1:T(8,128)(2,1)} fusion(bf16[768,1,1,512]{0,3,2,1:T(8,128)(2,1)S(1)} %copy-done.5, bf16[768,1,1,512]{0,3,2,1:T(8,128)(2,1)S(1)} %get-tuple-element.12, bf16[768,1,1,512]{0,3,2,1:T(8,128)(2,1)S(1)} %get-tuple-element.11, bf16[768,1,1,512]{0,3,2,1:T(8,128)(2,1)S(1)} %copy-done.4, ...), kind=kLoop, calls=%fused_computation | loop fusion | flops 51904512 | bytes 18874368 | tf_op jit(solution)/shard_map/stack | solution.py:66
  136.8 16.5 %copy.35 = bf16[768,4,3,512]{3,1,2,0:T(4,128)(2,1)} copy(bf16[768,4,3,512]{0,3,2,1:T(8,128)(2,1)} %maximum_maximum_fusion) | data formatting | bytes 18874368 | tf_op jit(solution)/shard_map/stack | solution.py:66
  (45 shorter events, 0.1 us)
Async XLA Ops:
  0.0 27.7 %copy-start = (bf16[120,768]{1,0:T(8,128)(2,1)S(1)}, bf16[120,768]{1,0:T(8,128)(2,1)}, u32[]{:S(2)}) copy-start(bf16[120,768]{1,0:T(8,128)(2,1)} %param.5) | copy-start | bytes 552964
  0.0 26.0 %collective-permute-start.2 = (bf16[1,3,512]{2,1,0:T(4,128)(2,1)}, bf16[1,3,512]{2,1,0:T(4,128)(2,1)S(1)}, u32[]{:S(2)}, u32[]{:S(2)}) collective-permute-start(bf16[1,3,512]{2,1,0:T(4,128)(2,1)} %bitcast.532), channel_id=1, source_target_pairs={{28,0},{0,4},{4,8},{8,12},{12,16},{16,20},{20,24},{24,28},{29,1},{... | collective-permute-start | bytes 9224 | tf_op jit(solution)/shard_map/ppermute | solution.py:16
  4.5 32.3 %collective-permute-start = (bf16[1,24,512]{2,1,0:T(8,128)(2,1)S(1)}, bf16[1,24,512]{2,1,0:T(8,128)(2,1)S(1)}, u32[]{:S(2)}, u32[]{:S(2)}) collective-permute-start(bf16[1,24,512]{2,1,0:T(8,128)(2,1)S(1)} %fusion.99), channel_id=1, source_target_pairs={{28,0},{0,4},{4,8},{8,12},{12,16},{16,20},{20,24},{24,28},{29,1},{... | collective-permute-start | bytes 73736 | tf_op jit(solution)/shard_map/ppermute | solution.py:16
  12.6 11.6 %copy-start.9 = (bf16[120,3,512]{2,0,1:T(8,128)(2,1)S(1)}, bf16[120,3,512]{2,0,1:T(8,128)(2,1)}, u32[]{:S(2)}) copy-start(bf16[120,3,512]{2,0,1:T(8,128)(2,1)} %param.7) | copy-start | bytes 1105924
  20.6 5.4 %copy-start.11 = (bf16[3,512]{1,0:T(4,128)(2,1)S(1)}, bf16[3,512]{1,0:T(4,128)(2,1)}, u32[]{:S(2)}) copy-start(bf16[3,512]{1,0:T(4,128)(2,1)} %param.8) | copy-start | bytes 9220
  20.6 18.0 %all-to-all-start = ((bf16[4,2,27648]{2,1,0:T(2,128)(2,1)}), bf16[4,2,27648]{2,1,0:T(2,128)(2,1)S(1)}, u32[]{:S(2)}, u32[]{:S(2)}) async-start(bf16[4,2,27648]{2,1,0:T(2,128)(2,1)} %reshape.289), calls=%async_computation | async-start | bytes 884736 | tf_op jit(solution)/shard_map/all_to_all | solution.py:45
  24.2 58.3 %collective-permute-start.1 = (bf16[1,120,3,512]{3,1,2,0:T(8,128)(2,1)S(1)}, bf16[1,120,3,512]{3,1,2,0:T(8,128)(2,1)S(1)}, u32[]{:S(2)}, u32[]{:S(2)}) collective-permute-start(bf16[1,120,3,512]{3,1,2,0:T(8,128)(2,1)S(1)} %bitcast.530), channel_id=1, source_target_pairs={{28,0},{0,4},{4,8},{8,12},{12,16},{16,20},{20,24},{24,28},{29,1},{... | collective-permute-start | bytes 1105928 | tf_op jit(solution)/shard_map/ppermute | solution.py:16
  26.0 10.7 %collective-permute-start.5 = (bf16[2,3,512]{2,1,0:T(4,128)(2,1)S(1)}, bf16[2,3,512]{2,1,0:T(4,128)(2,1)S(1)}, u32[]{:S(2)}, u32[]{:S(2)}) collective-permute-start(bf16[2,3,512]{2,1,0:T(4,128)(2,1)S(1)} %pad_maximum_fusion.2), channel_id=1, source_target_pairs={{24,0},{28,4},{0,8},{4,12},{8,16},{12,20},{16,24},{20,28},{25,1},{... | collective-permute-start | bytes 18440 | tf_op jit(solution)/shard_map/ppermute | solution.py:16
  36.8 18.9 %collective-permute-start.3 = (bf16[2,24,512]{2,1,0:T(8,128)(2,1)S(1)}, bf16[2,24,512]{2,1,0:T(8,128)(2,1)S(1)}, u32[]{:S(2)}, u32[]{:S(2)}) collective-permute-start(bf16[2,24,512]{2,1,0:T(8,128)(2,1)S(1)} %pad_maximum_fusion.1), channel_id=1, source_target_pairs={{24,0},{28,4},{0,8},{4,12},{8,16},{12,20},{16,24},{20,28},{25,1},{... | collective-permute-start | bytes 147464 | tf_op jit(solution)/shard_map/ppermute | solution.py:16
  46.1 6.9 %copy-start.10 = (bf16[24,512]{1,0:T(8,128)(2,1)S(1)}, bf16[24,512]{1,0:T(8,128)(2,1)}, u32[]{:S(2)}) copy-start(bf16[24,512]{1,0:T(8,128)(2,1)} %param.9) | copy-start | bytes 73732
  63.8 16.1 %slice-start.5 = ((s8[4718592]{0:T(1024)(128)(4,1)}), s8[4194304]{0:T(1024)(128)(4,1)S(1)}, s32[]{:S(2)}) async-start(s8[4718592]{0:T(1024)(128)(4,1)} %bitcast.513), calls=%async_computation.6 | async-start | bytes 8388608
  71.8 8.0 %slice-start.6 = ((s8[4718592]{0:T(1024)(128)(4,1)}), s8[524288]{0:T(1024)(128)(4,1)S(1)}, s32[]{:S(2)}) async-start(s8[4718592]{0:T(1024)(128)(4,1)} %bitcast.513), calls=%async_computation.7 | async-start | bytes 1048576
  83.5 20.7 %collective-permute-start.4 = (bf16[2,120,3,512]{3,1,2,0:T(8,128)(2,1)}, bf16[2,120,3,512]{3,1,2,0:T(8,128)(2,1)}, u32[]{:S(2)}, u32[]{:S(2)}) collective-permute-start(bf16[2,120,3,512]{3,1,2,0:T(8,128)(2,1)} %pad_maximum_fusion), channel_id=1, source_target_pairs={{24,0},{28,4},{0,8},{4,12},{8,16},{12,20},{16,24},{20,28},{25,1},{... | collective-permute-start | bytes 2211848 | tf_op jit(solution)/shard_map/ppermute | solution.py:16
  93.0 5.8 %copy-start.1 = (f32[768,1536]{0,1:T(8,128)S(1)}, f32[768,1536]{0,1:T(8,128)}, u32[]{:S(2)}) copy-start(f32[768,1536]{0,1:T(8,128)} %copy.32) | copy-start | bytes 14155780
  110.0 1.8 %copy-start.8 = (bf16[1,120,3,512]{1,3,2,0:T(8,128)(2,1)S(1)}, bf16[1,120,3,512]{1,3,2,0:T(8,128)(2,1)}, u32[]{:S(2)}) copy-start(bf16[1,120,3,512]{1,3,2,0:T(8,128)(2,1)} %copy.34) | copy-start | bytes 1105924
  112.6 14.0 %slice-start = ((s8[18874368]{0:T(1024)(128)(4,1)}), s8[4194304]{0:T(1024)(128)(4,1)S(1)}, s32[]{:S(2)}) async-start(s8[18874368]{0:T(1024)(128)(4,1)} %bitcast.511), calls=%async_computation.1 | async-start | bytes 8388608
  112.6 14.0 %slice-start.1 = ((s8[18874368]{0:T(1024)(128)(4,1)}), s8[4194304]{0:T(1024)(128)(4,1)S(1)}, s32[]{:S(2)}) async-start(s8[18874368]{0:T(1024)(128)(4,1)} %bitcast.511), calls=%async_computation.2 | async-start | bytes 8388608
  112.6 14.0 %slice-start.2 = ((s8[18874368]{0:T(1024)(128)(4,1)}), s8[4194304]{0:T(1024)(128)(4,1)S(1)}, s32[]{:S(2)}) async-start(s8[18874368]{0:T(1024)(128)(4,1)} %bitcast.511), calls=%async_computation.3 | async-start | bytes 8388608
  119.2 7.6 %slice-start.3 = ((s8[18874368]{0:T(1024)(128)(4,1)}), s8[4194304]{0:T(1024)(128)(4,1)S(1)}, s32[]{:S(2)}) async-start(s8[18874368]{0:T(1024)(128)(4,1)} %bitcast.511), calls=%async_computation.4 | async-start | bytes 8388608
  119.3 8.5 %slice-start.4 = ((s8[18874368]{0:T(1024)(128)(4,1)}), s8[2097152]{0:T(1024)(128)(4,1)S(1)}, s32[]{:S(2)}) async-start(s8[18874368]{0:T(1024)(128)(4,1)} %bitcast.511), calls=%async_computation.5 | async-start | bytes 4194304
  127.8 1.2 copy-start.2
  127.8 1.4 copy-start.3
  127.8 1.6 %copy-start.4 = (bf16[768,1,1,512]{0,3,2,1:T(8,128)(2,1)S(1)}, bf16[768,1,1,512]{0,3,2,1:T(8,128)(2,1)}, u32[]{:S(2)}) copy-start(bf16[768,1,1,512]{0,3,2,1:T(8,128)(2,1)} %get-tuple-element.17) | copy-start | bytes 2359300
  127.8 1.8 %copy-start.5 = (bf16[768,1,1,512]{0,3,2,1:T(8,128)(2,1)S(1)}, bf16[768,1,1,512]{0,3,2,1:T(8,128)(2,1)}, u32[]{:S(2)}) copy-start(bf16[768,1,1,512]{0,3,2,1:T(8,128)(2,1)} %get-tuple-element.18) | copy-start | bytes 2359300
  127.8 2.1 %copy-start.6 = (bf16[768,1,1,512]{0,3,2,1:T(8,128)(2,1)S(1)}, bf16[768,1,1,512]{0,3,2,1:T(8,128)(2,1)}, u32[]{:S(2)}) copy-start(bf16[768,1,1,512]{0,3,2,1:T(8,128)(2,1)} %fusion.86) | copy-start | bytes 2359300
  127.8 2.3 %copy-start.7 = (bf16[768,1,1,512]{0,3,2,1:T(8,128)(2,1)S(1)}, bf16[768,1,1,512]{0,3,2,1:T(8,128)(2,1)}, u32[]{:S(2)}) copy-start(bf16[768,1,1,512]{0,3,2,1:T(8,128)(2,1)} %fusion.89) | copy-start | bytes 2359300
where the time goes:
time: 154 us; the launch traced here: 153 us
  local copies, waits for them, and re-layouts  66 us (43%)
  other arithmetic  38.1 us (25%)
  matrix products  35.5 us (23%)
  starting transfers between devices  13.4 us (9%)
    another operation x7, other arithmetic, skin_block(): return jnp.stack(positions, axis=1).astype(jnp.bfloat16)  28.9 us
    dot_general x4, matrix products, skin_block(): jnp.einsum('mjr,jv->mrv', joint_poses, weight_block, preferred_element_ty...  26.9 us
    unnamed x42, local copies, waits for them, and re-layouts  24.4 us
    another operation x1, local copies, waits for them, and re-layouts, per_device(): return jnp.stack(outputs, axis=1)  16.5 us
    add x2, local copies, waits for them, and re-layouts, skin_block(): shaped = shaped + template_block.reshape(1, -1).astype(jnp.float32)  12.1 us
    ppermute x6, starting transfers between devices, passed_along(): return lax.ppermute(block, axis, route)  9.8 us
    dot_general x4, matrix products, skin_block(): lax.dot_general(coefficients, flattened, (((0,), (0,)), ((), ())), prefer...  8.62 us
    all_to_all x2, local copies, waits for them, and re-layouts, per_device(): lax.all_to_all(transforms, 'batch', split_axis=2, concat_axis=1, tiled=True)  6.89 us
  transfers between devices with their start and end apart: 7, of which 0 were waited for; matrix products, arithmetic and copies ran while one was open for 58% of the time, Pallas kernels for 0%

commit v1 on v0

v1 whole, which is shorter than its diff:
```python
import functools
import jax
import jax.numpy as jnp
from jax import lax
from jax.experimental import pallas as pl
from jax.experimental.pallas import tpu as pltpu
from jax.sharding import PartitionSpec as P

STEPS = 4
LANES = 128
BF16 = jnp.bfloat16
F32 = jnp.float32


def exchange_kernel(
    n_blk, n_batch, tr_ref, ba_ref, te_ref, we_ref,
    tr_out, ba_out, te_out, we_out,
    stage, tr_send, tr_recv, bl_send, bl_recv, fw_send, fw_recv, own_sem,
):
    blk, bat = lax.axis_index("blk"), lax.axis_index("batch")
    sibling = bat + 1 - 2 * lax.rem(bat, 2)
    chars = tr_out.shape[3]
    half = ba_ref.shape[2] // 2
    hop = STEPS - 1

    own = pltpu.make_async_copy(
        tr_ref.at[:, :, pl.ds(pl.multiple_of(bat * chars, LANES), chars)], stage, own_sem.at[0]
    )
    own.start()

    partners = [lax.rem(bat + i, n_batch) for i in range(1, n_batch)]
    ahead = [lax.rem(blk + i, n_blk) for i in range(1, hop + 1)]
    behind = [lax.rem(blk + n_blk - i, n_blk) for i in range(1, hop + 1)]
    barrier = pltpu.get_barrier_semaphore()
    for q in partners:
        pl.semaphore_signal(barrier, inc=1, device_id={"blk": blk, "batch": q})
    for b in ahead + behind:
        pl.semaphore_signal(barrier, inc=1, device_id={"blk": b, "batch": bat})
    pl.semaphore_wait(barrier, len(partners) + 2 * hop)

    mine = pl.ds(pl.multiple_of(lax.rem(bat, 2) * half, LANES), half)
    arrays = ((ba_ref, ba_out), (te_ref, te_out), (we_ref, we_out))

    moves = []
    for i, q in enumerate(partners):
        moves.append(pltpu.make_async_remote_copy(
            src_ref=tr_ref.at[:, :, pl.ds(pl.multiple_of(q * chars, LANES), chars)],
            dst_ref=tr_out.at[bat],
            send_sem=tr_send.at[i], recv_sem=tr_recv.at[i],
            device_id={"blk": blk, "batch": q},
        ))
    blocks = []
    for i, b in enumerate(ahead):
        for k, (src, dst) in enumerate(arrays):
            lead = (slice(None),) * (len(src.shape) - 1)
            blocks.append(pltpu.make_async_remote_copy(
                src_ref=src.at[lead + (mine,)], dst_ref=dst.at[(i,) + lead + (mine,)],
                send_sem=bl_send.at[i, k], recv_sem=bl_recv.at[i, k],
                device_id={"blk": b, "batch": bat},
            ))
    for c in moves + blocks:
        c.start()
    own.wait()
    put = pltpu.make_async_copy(stage, tr_out.at[bat], own_sem.at[1])
    put.start()
    passes = []
    for i in range(hop):
        for k, (src, dst) in enumerate(arrays):
            lead = (i,) + (slice(None),) * (len(src.shape) - 1)
            blocks[3 * i + k].wait_recv()
            c = pltpu.make_async_remote_copy(
                src_ref=dst.at[lead + (mine,)], dst_ref=dst.at[lead + (mine,)],
                send_sem=fw_send.at[i, k], recv_sem=fw_recv.at[i, k],
                device_id={"blk": blk, "batch": sibling},
            )
            c.start()
            passes.append(c)
    put.wait()
    for c in blocks:
        c.wait_send()
    for c in moves + passes:
        c.wait()


def exchange(n_blk, n_batch, transforms, basis, template, weights):
    m, jl, total = transforms.shape
    chars = total // n_batch
    hop = STEPS - 1
    any_spec = pl.BlockSpec(memory_space=pl.ANY)
    dma = pltpu.SemaphoreType.DMA
    return pl.pallas_call(
        functools.partial(exchange_kernel, n_blk, n_batch),
        out_shape=(
            jax.ShapeDtypeStruct((n_batch, m, jl, chars), BF16),
            jax.ShapeDtypeStruct((hop,) + basis.shape, BF16),
            jax.ShapeDtypeStruct((hop,) + template.shape, BF16),
            jax.ShapeDtypeStruct((hop,) + weights.shape, BF16),
        ),
        in_specs=[any_spec] * 4,
        out_specs=(any_spec,) * 4,
        scratch_shapes=[
            pltpu.VMEM((m, jl, chars), BF16),
            dma((n_batch - 1,)), dma((n_batch - 1,)),
            dma((hop, 3)), dma((hop, 3)), dma((hop, 3)), dma((hop, 3)), dma((2,)),
        ],
        compiler_params=pltpu.CompilerParams(
            collective_id=0, has_side_effects=True, vmem_limit_bytes=4 << 20
        ),
        name="exchange",
    )(transforms, basis, template, weights)


def skin_kernel(
    co_ref, tr_ref, ba0_ref, te0_ref, we0_ref, ba_ref, te_ref, we_ref, out_ref,
    basis, weights, mixed, poses, coefs,
):
    rows = co_ref.shape[1]
    k = co_ref.shape[0]
    depth = basis.shape[2]
    comps = poses.shape[0]
    joints = weights.shape[1]
    verts = we0_ref.shape[1]
    tiles = verts // LANES
    wide = 2 * LANES

    @pl.when(pl.program_id(0) == 0)
    def _():
        for s in range(STEPS):
            w = (we0_ref[...] if s == 0 else we_ref[s - 1]).astype(F32)
            weights[s] = (w / jnp.sum(w, axis=0, keepdims=True)).astype(BF16)
            te = te0_ref[...] if s == 0 else te_ref[s - 1]
            for e in range(3):
                basis[s, e, :k] = ba0_ref[e] if s == 0 else ba_ref[s - 1, e]
                row = te[e:e + 1].astype(F32)
                pad = jnp.broadcast_to(row, (depth - k, verts))
                first = lax.broadcasted_iota(jnp.int32, (depth - k, verts), 0) == 0
                basis[s, e, k:] = jnp.where(first, pad, 0.0).astype(BF16)

    ones = jnp.where(
        lax.broadcasted_iota(jnp.int32, (depth - k, rows), 0) == 0, 1.0, 0.0
    ).astype(F32)
    padded = jnp.concatenate([co_ref[...].astype(F32), ones], axis=0)
    coefs[...] = padded.T.astype(BF16)
    for m in range(comps):
        parts = [tr_ref[i, m].astype(F32) for i in range(tr_ref.shape[0])]
        poses[m] = jnp.concatenate(parts, axis=0).T.astype(BF16)

    period = 3 * tiles * STEPS
    for s in range(STEPS):
        for n in range(verts // wide):
            cols = slice(n * wide, (n + 1) * wide)
            w = weights[s, :, cols]
            shaped = [
                jnp.dot(coefs[...], basis[s, e, :, cols], preferred_element_type=F32)
                for e in range(3)
            ]
            for d in range(3):
                total = jnp.dot(poses[4 * d + 3], w, preferred_element_type=F32)
                for e in range(3):
                    total = total + shaped[e] * jnp.dot(
                        poses[4 * d + e], w, preferred_element_type=F32
                    )
                for h in range(wide // LANES):
                    at = (d * tiles + n * (wide // LANES) + h) * STEPS + s
                    mixed[pl.ds(at, rows, stride=period), :] = total[:, h * LANES:(h + 1) * LANES]
    out_ref[...] = mixed[...].astype(BF16)


def skin(coefficients, poses, basis, template, weights, basis_in, template_in, weights_in):
    k, chars = coefficients.shape
    n_batch, comps, jl, _ = poses.shape
    verts = weights.shape[1]
    joints = weights.shape[0]
    rows = LANES
    depth = -(-(k + 1) // 8) * 8
    period = 3 * (verts // LANES) * STEPS

    def whole(a):
        return pl.BlockSpec(a.shape, lambda i: (0,) * a.ndim)

    out = pl.pallas_call(
        skin_kernel,
        grid=(chars // rows,),
        out_shape=jax.ShapeDtypeStruct((chars * period, LANES), BF16),
        in_specs=[
            pl.BlockSpec((k, rows), lambda i: (0, i)),
            pl.BlockSpec((n_batch, comps, jl, rows), lambda i: (0, 0, 0, i)),
            whole(basis), whole(template), whole(weights),
            whole(basis_in), whole(template_in), whole(weights_in),
        ],
        out_specs=pl.BlockSpec((rows * period, LANES), lambda i: (i, 0)),
        scratch_shapes=[
            pltpu.VMEM((STEPS, 3, depth, verts), BF16),
            pltpu.VMEM((STEPS, joints, verts), BF16),
            pltpu.VMEM((rows * period, LANES), F32),
            pltpu.VMEM((comps, rows, joints), BF16),
            pltpu.VMEM((rows, depth), BF16),
        ],
        compiler_params=pltpu.CompilerParams(
            dimension_semantics=("arbitrary",), vmem_limit_bytes=48 << 20
        ),
        name="skin",
    )(coefficients, poses, basis, template, weights, basis_in, template_in, weights_in)
    out = out.reshape(chars, 3, verts // LANES, STEPS, LANES)
    return out.transpose(0, 3, 1, 2, 4).reshape(chars, STEPS, 3, verts)


def solution(mesh):
    n_blk, n_batch = mesh.shape["blk"], mesh.shape["batch"]

    def per_device(coefficients, transforms, basis, template, skin_weights):
        basis = jnp.transpose(basis, (1, 0, 2))
        poses, basis_in, template_in, weights_in = exchange(
            n_blk, n_batch, transforms, basis, template, skin_weights
        )
        return skin(
            coefficients, poses, basis, template, skin_weights,
            basis_in, template_in, weights_in,
        )

    in_specs = (
        P(None, ("blk", "batch")),
        P(None, "batch", "blk"),
        P(None, None, "blk"),
        P(None, "blk"),
        P(None, "blk"),
    )
    out_specs = P(("blk", "batch"), None, None, None)
    return jax.shard_map(
        per_device, mesh=mesh, in_specs=in_specs, out_specs=out_specs, check_vma=False
    )
```

time: 154 us -> 51.4 us (0.33)
  local copies, waits for them, and re-layouts: 66 us -> 6.8 us
  Pallas kernels: 0 us -> 44.1 us
  other arithmetic: 38.1 us -> 0 us
  matrix products: 35.5 us -> 0 us
  starting transfers between devices: 13.4 us -> 0 us
    pallas_call x0 -> x2, Pallas kernels: none -> 44.1 us  [the longest x1 25.9 us: exchange(): pl.pallas_call(functools.partial(exchange_kernel, n_blk, n_batch), out_sh...]
    another operation x8 -> x0, other arithmetic: 35.6 us -> none  [the longest x7 28.9 us: skin_block(): return jnp.stack(positions, axis=1).astype(jnp.bfloat16)]
    dot_general x8 -> x0, matrix products: 35.5 us -> none  [the longest x4 26.9 us: skin_block(): jnp.einsum('mjr,jv->mrv', joint_poses, weight_block, preferred_element_ty...]
    unnamed x42 -> x16, local copies, waits for them, and re-layouts: 24.4 us -> 6.8 us
    another operation x1 -> x0, local copies, waits for them, and re-layouts: 16.5 us -> none  [per_device(): return jnp.stack(outputs, axis=1)]
    add x2 -> x0, local copies, waits for them, and re-layouts: 12.1 us -> none  [skin_block(): shaped = shaped + template_block.reshape(1, -1).astype(jnp.float32)]
    ppermute x6 -> x0, starting transfers between devices: 9.8 us -> none  [passed_along(): return lax.ppermute(block, axis, route)]
    all_to_all x2 -> x0, local copies, waits for them, and re-layouts: 6.89 us -> none  [per_device(): lax.all_to_all(transforms, 'batch', split_axis=2, concat_axis=1, tiled=True)]
  transfers between devices with their start and end apart: 7 -> 0, of which waited for: 0 -> 0; matrix products, arithmetic and copies ran while one was open for 58% -> 0% of each run, Pallas kernels for 0% -> 0%
where the time goes in v1:
time: 51.4 us; the launch traced here: 51 us
  Pallas kernels  44.1 us (86%)
  local copies, waits for them, and re-layouts  6.8 us (13%)
    pallas_call x1, Pallas kernels, exchange(): pl.pallas_call(functools.partial(exchange_kernel, n_blk, n_batch), out_sh...  25.9 us
    pallas_call x1, Pallas kernels, skin(): pl.pallas_call(skin_kernel, grid=(chars // rows,), out_shape=jax.ShapeDty...  18.3 us
    unnamed x16, local copies, waits for them, and re-layouts  6.8 us

profile of v1, /device:TPU:0, one launch (start us, length us, event | category | flops | bytes accessed | tf_op | source)
XLA Modules:
  0.0 51.0 jit_solution(1879744959822137410)
XLA Ops:
  0.0 0.0 copy-start
  0.0 1.0 %copy-done = bf16[120,3,512]{2,0,1:T(8,128)(2,1)S(1)} copy-done((bf16[120,3,512]{2,0,1:T(8,128)(2,1)S(1)}, bf16[120,3,512]{2,0,1:T(8,128)(2,1)}, u32[]{:S(2)}) %copy-start) | copy-done | bytes 368664
  1.0 0.0 copy-start.2
  1.0 1.1 %copy-done.2 = bf16[12,6,3072]{2,1,0:T(8,128)(2,1)S(1)} copy-done((bf16[12,6,3072]{2,1,0:T(8,128)(2,1)S(1)}, bf16[12,6,3072]{2,1,0:T(8,128)(2,1)}, u32[]{:S(2)}) %copy-start.2) | copy-done | bytes 442392
  2.1 0.0 copy-start.4
  2.1 0.7 %copy-done.4 = bf16[24,512]{1,0:T(8,128)(2,1)S(1)} copy-done((bf16[24,512]{1,0:T(8,128)(2,1)S(1)}, bf16[24,512]{1,0:T(8,128)(2,1)}, u32[]{:S(2)}) %copy-start.4) | copy-done | bytes 24600
  2.8 0.0 copy-start.6
  2.8 0.7 %copy-done.6 = bf16[3,512]{1,0:T(4,128)(2,1)S(1)} copy-done((bf16[3,512]{1,0:T(4,128)(2,1)S(1)}, bf16[3,512]{1,0:T(4,128)(2,1)}, u32[]{:S(2)}) %copy-start.6) | copy-done | bytes 3096
  3.5 25.9 %exchange.1 = (bf16[4,12,6,768]{3,2,1,0:T(8,128)(2,1)S(1)}, bf16[3,3,120,512]{3,2,1,0:T(8,128)(2,1)S(1)}, bf16[3,3,512]{2,1,0:T(4,128)(2,1)S(1)}, bf16[3,24,512]{2,1,0:T(8,128)(2,1)S(1)}) custom-call(bf16[12,6,3072]{2,1,0:T(8,128)(2,1)S(1)} %copy-done.2, bf16[3,120,512]{2,1,0:T(8,128)(2,1)S(1)} %bitcast.6, bf16[3,512]{1,0:T(4,128)(2,1)S(1)} %copy-done.6, ...), custom_call_target="tpu_custom_call" | custom-call | tf_op jit(solution)/shard_map/exchange/pallas_call | solution.py:91
  29.3 0.0 copy-start.1
  29.4 1.0 %copy-done.1 = bf16[120,3,512]{2,0,1:T(8,128)(2,1)S(1)} copy-done((bf16[120,3,512]{2,0,1:T(8,128)(2,1)S(1)}, bf16[120,3,512]{2,0,1:T(8,128)(2,1)}, u32[]{:S(2)}) %copy-start.1) | copy-done | bytes 368664
  30.3 0.0 copy-start.3
  30.3 0.9 %copy-done.3 = bf16[120,768]{1,0:T(8,128)(2,1)S(1)} copy-done((bf16[120,768]{1,0:T(8,128)(2,1)S(1)}, bf16[120,768]{1,0:T(8,128)(2,1)}, u32[]{:S(2)}) %copy-start.3) | copy-done | bytes 184344
  31.3 0.0 copy-start.5
  31.3 0.7 %copy-done.5 = bf16[24,512]{1,0:T(8,128)(2,1)S(1)} copy-done((bf16[24,512]{1,0:T(8,128)(2,1)S(1)}, bf16[24,512]{1,0:T(8,128)(2,1)}, u32[]{:S(2)}) %copy-start.5) | copy-done | bytes 24600
  32.0 0.0 copy-start.7
  32.0 0.7 %copy-done.7 = bf16[3,512]{1,0:T(4,128)(2,1)S(1)} copy-done((bf16[3,512]{1,0:T(4,128)(2,1)S(1)}, bf16[3,512]{1,0:T(4,128)(2,1)}, u32[]{:S(2)}) %copy-start.7) | copy-done | bytes 3096
  32.7 18.3 %skin.1 = bf16[36864,128]{1,0:T(8,128)(2,1)} custom-call(bf16[120,768]{1,0:T(8,128)(2,1)S(1)} %copy-done.3, bf16[4,12,6,768]{3,2,1,0:T(8,128)(2,1)S(1)} %get-tuple-element.9.tr_ref, bf16[3,120,512]{2,1,0:T(8,128)(2,1)S(1)} %bitcast.7, bf16[3,512]{1,0:T(4,128)(2,1)S(1)} %copy-done.7, bf16[24,512]{1,0:T(8,128)(2,1)S(1)} %copy-done.5, ...), custom_call_target="tpu_custom_call" | custom-call | tf_op jit(solution)/shard_map/skin/pallas_call | solution.py:181
Async XLA Ops:
  0.0 1.0 %copy-start = (bf16[120,3,512]{2,0,1:T(8,128)(2,1)S(1)}, bf16[120,3,512]{2,0,1:T(8,128)(2,1)}, u32[]{:S(2)}) copy-start(bf16[120,3,512]{2,0,1:T(8,128)(2,1)} %param.7) | copy-start | bytes 1105924
  1.0 1.1 %copy-start.2 = (bf16[12,6,3072]{2,1,0:T(8,128)(2,1)S(1)}, bf16[12,6,3072]{2,1,0:T(8,128)(2,1)}, u32[]{:S(2)}) copy-start(bf16[12,6,3072]{2,1,0:T(8,128)(2,1)} %tr_ref.1) | copy-start | bytes 1327108
  2.1 0.7 %copy-start.4 = (bf16[24,512]{1,0:T(8,128)(2,1)S(1)}, bf16[24,512]{1,0:T(8,128)(2,1)}, u32[]{:S(2)}) copy-start(bf16[24,512]{1,0:T(8,128)(2,1)} %we0_ref.1) | copy-start | bytes 73732
  2.8 0.7 %copy-start.6 = (bf16[3,512]{1,0:T(4,128)(2,1)S(1)}, bf16[3,512]{1,0:T(4,128)(2,1)}, u32[]{:S(2)}) copy-start(bf16[3,512]{1,0:T(4,128)(2,1)} %te0_ref.1) | copy-start | bytes 9220
  29.3 1.0 %copy-start.1 = (bf16[120,3,512]{2,0,1:T(8,128)(2,1)S(1)}, bf16[120,3,512]{2,0,1:T(8,128)(2,1)}, u32[]{:S(2)}) copy-start(bf16[120,3,512]{2,0,1:T(8,128)(2,1)} %param.7) | copy-start | bytes 1105924
  30.3 0.9 %copy-start.3 = (bf16[120,768]{1,0:T(8,128)(2,1)S(1)}, bf16[120,768]{1,0:T(8,128)(2,1)}, u32[]{:S(2)}) copy-start(bf16[120,768]{1,0:T(8,128)(2,1)} %co_ref.1) | copy-start | bytes 552964
  31.3 0.7 %copy-start.5 = (bf16[24,512]{1,0:T(8,128)(2,1)S(1)}, bf16[24,512]{1,0:T(8,128)(2,1)}, u32[]{:S(2)}) copy-start(bf16[24,512]{1,0:T(8,128)(2,1)} %we0_ref.1) | copy-start | bytes 73732
  32.0 0.7 %copy-start.7 = (bf16[3,512]{1,0:T(4,128)(2,1)S(1)}, bf16[3,512]{1,0:T(4,128)(2,1)}, u32[]{:S(2)}) copy-start(bf16[3,512]{1,0:T(4,128)(2,1)} %te0_ref.1) | copy-start | bytes 9220

commit v2 on v1

--- a/solution.py
+++ b/solution.py
@@ -19,9 +19,12 @@
 ):
     blk, bat = lax.axis_index("blk"), lax.axis_index("batch")
     sibling = bat + 1 - 2 * lax.rem(bat, 2)
+    odd = lax.rem(blk, 2)
+    pair = blk + 1 - 2 * odd
+    after = lax.rem(blk + 2, n_blk)
+    before = lax.rem(blk + n_blk - 2, n_blk)
     chars = tr_out.shape[3]
     half = ba_ref.shape[2] // 2
-    hop = STEPS - 1
 
     own = pltpu.make_async_copy(
         tr_ref.at[:, :, pl.ds(pl.multiple_of(bat * chars, LANES), chars)], stage, own_sem.at[0]
@@ -29,17 +32,44 @@
     own.start()
 
     partners = [lax.rem(bat + i, n_batch) for i in range(1, n_batch)]
-    ahead = [lax.rem(blk + i, n_blk) for i in range(1, hop + 1)]
-    behind = [lax.rem(blk + n_blk - i, n_blk) for i in range(1, hop + 1)]
     barrier = pltpu.get_barrier_semaphore()
     for q in partners:
         pl.semaphore_signal(barrier, inc=1, device_id={"blk": blk, "batch": q})
-    for b in ahead + behind:
+    for b in (pair, after, before):
         pl.semaphore_signal(barrier, inc=1, device_id={"blk": b, "batch": bat})
-    pl.semaphore_wait(barrier, len(partners) + 2 * hop)
+    pl.semaphore_wait(barrier, len(partners) + 3)
 
     mine = pl.ds(pl.multiple_of(lax.rem(bat, 2) * half, LANES), half)
     arrays = ((ba_ref, ba_out), (te_ref, te_out), (we_ref, we_out))
+
+    def hop(slot_from, slot_to, where, send, recv, target):
+        made = []
+        for k, (src, dst) in enumerate(arrays):
+            lead = (slice(None),) * (len(src.shape) - 1)
+            part = src.at[lead + (mine,)] if slot_from == 0 else dst.at[(slot_from - 1,) + lead + (mine,)]
+            made.append(pltpu.make_async_remote_copy(
+                src_ref=part, dst_ref=dst.at[(slot_to - 1,) + lead + (mine,)],
+                send_sem=send.at[where, k], recv_sem=recv.at[slot_to - 1, k],
+                device_id={"blk": target[0], "batch": target[1]},
+            ))
+        return made
+
+    def start(copies):
+        for c in copies:
+            c.start()
+
+    def arrived(slot):
+        for c in hop(slot, slot, slot - 1, bl_send, bl_recv, (pair, bat)):
+            c.wait_recv()
+
+    def share(slot):
+        start(hop(slot, slot, slot - 1, fw_send, fw_recv, (blk, sibling)))
+
+    start(hop(0, 2, 1, bl_send, bl_recv, (after, bat)))
+
+    @pl.when(odd == 0)
+    def _():
+        start(hop(0, 1, 0, bl_send, bl_recv, (pair, bat)))
 
     moves = []
     for i, q in enumerate(partners):
@@ -49,44 +79,53 @@
             send_sem=tr_send.at[i], recv_sem=tr_recv.at[i],
             device_id={"blk": blk, "batch": q},
         ))
-    blocks = []
-    for i, b in enumerate(ahead):
-        for k, (src, dst) in enumerate(arrays):
-            lead = (slice(None),) * (len(src.shape) - 1)
-            blocks.append(pltpu.make_async_remote_copy(
-                src_ref=src.at[lead + (mine,)], dst_ref=dst.at[(i,) + lead + (mine,)],
-                send_sem=bl_send.at[i, k], recv_sem=bl_recv.at[i, k],
-                device_id={"blk": b, "batch": bat},
-            ))
-    for c in moves + blocks:
-        c.start()
+    start(moves)
     own.wait()
     put = pltpu.make_async_copy(stage, tr_out.at[bat], own_sem.at[1])
     put.start()
-    passes = []
-    for i in range(hop):
-        for k, (src, dst) in enumerate(arrays):
-            lead = (i,) + (slice(None),) * (len(src.shape) - 1)
-            blocks[3 * i + k].wait_recv()
-            c = pltpu.make_async_remote_copy(
-                src_ref=dst.at[lead + (mine,)], dst_ref=dst.at[lead + (mine,)],
-                send_sem=fw_send.at[i, k], recv_sem=fw_recv.at[i, k],
-                device_id={"blk": blk, "batch": sibling},
-            )
-            c.start()
-            passes.append(c)
+
+    arrived(2)
+
+    @pl.when(odd == 0)
+    def _():
+        start(hop(2, 3, 2, bl_send, bl_recv, (pair, bat)))
+
+    @pl.when(odd == 1)
+    def _():
+        start(hop(2, 1, 0, bl_send, bl_recv, (pair, bat)))
+
+    share(2)
+    arrived(1)
+
+    @pl.when(odd == 0)
+    def _():
+        start(hop(1, 3, 3, bl_send, bl_recv, (after, bat)))
+
+    share(1)
+    arrived(3)
+    share(3)
     put.wait()
-    for c in blocks:
+    for c in moves:
+        c.wait()
+    for slot in (2, 1, 3):
+        for c in hop(slot, slot, slot - 1, fw_send, fw_recv, (blk, sibling)):
+            c.wait()
+    for c in hop(0, 2, 1, bl_send, bl_recv, (after, bat)) + hop(0, 1, 0, bl_send, bl_recv, (pair, bat)):
         c.wait_send()
-    for c in moves + passes:
-        c.wait()
+
+    @pl.when(odd == 0)
+    def _():
+        for c in hop(2, 3, 2, bl_send, bl_recv, (pair, bat)) + hop(1, 3, 3, bl_send, bl_recv, (after, bat)):
+            c.wait_send()
 
 
 def exchange(n_blk, n_batch, transforms, basis, template, weights):
     m, jl, total = transforms.shape
     chars = total // n_batch
     hop = STEPS - 1
+    assert n_blk % 2 == 0 and n_blk > STEPS and n_batch % 2 == 0 and STEPS == 4
     any_spec = pl.BlockSpec(memory_space=pl.ANY)
+    hbm_spec = pl.BlockSpec(memory_space=pl.ANY)
     dma = pltpu.SemaphoreType.DMA
     return pl.pallas_call(
         functools.partial(exchange_kernel, n_blk, n_batch),
@@ -96,16 +135,17 @@
             jax.ShapeDtypeStruct((hop,) + template.shape, BF16),
             jax.ShapeDtypeStruct((hop,) + weights.shape, BF16),
         ),
-        in_specs=[any_spec] * 4,
+        in_specs=[hbm_spec] * 4,
         out_specs=(any_spec,) * 4,
         scratch_shapes=[
             pltpu.VMEM((m, jl, chars), BF16),
             dma((n_batch - 1,)), dma((n_batch - 1,)),
-            dma((hop, 3)), dma((hop, 3)), dma((hop, 3)), dma((hop, 3)), dma((2,)),
+            dma((hop + 1, 3)), dma((hop, 3)), dma((hop, 3)), dma((hop, 3)), dma((2,)),
         ],
         compiler_params=pltpu.CompilerParams(
-            collective_id=0, has_side_effects=True, vmem_limit_bytes=4 << 20
+            collective_id=0, has_side_effects=True, vmem_limit_bytes=67043328
         ),
+        cost_estimate=pl.CostEstimate(flops=0, bytes_accessed=20 << 20, transcendentals=0),
         name="exchange",
     )(transforms, basis, template, weights)
 
@@ -197,7 +237,7 @@
             pltpu.VMEM((rows, depth), BF16),
         ],
         compiler_params=pltpu.CompilerParams(
-            dimension_semantics=("arbitrary",), vmem_limit_bytes=48 << 20
+            dimension_semantics=("arbitrary",), vmem_limit_bytes=67043328
         ),
         name="skin",
     )(coefficients, poses, basis, template, weights, basis_in, template_in, weights_in)

time: 51.4 us -> 44.9 us (0.87)
  local copies, waits for them, and re-layouts: 6.8 us -> 0 us
  Pallas kernels: 44.1 us -> 44.8 us
    unnamed x16 -> x0, local copies, waits for them, and re-layouts: 6.8 us -> none
    pallas_call x1, Pallas kernels: 18.3 us -> 19.7 us  [skin(): pl.pallas_call(skin_kernel, grid=(chars // rows,), out_shape=jax.ShapeDty...]
    pallas_call x1, Pallas kernels: 25.9 us -> 25.1 us  [exchange(): pl.pallas_call(functools.partial(exchange_kernel, n_blk, n_batch), out_sh...]
where the time goes in v2:
time: 44.9 us; the launch traced here: 44.8 us
  Pallas kernels  44.8 us (100%)
    pallas_call x1, Pallas kernels, exchange(): pl.pallas_call(functools.partial(exchange_kernel, n_blk, n_batch), out_sh...  25.1 us
    pallas_call x1, Pallas kernels, skin(): pl.pallas_call(skin_kernel, grid=(chars // rows,), out_shape=jax.ShapeDty...  19.7 us

profile of v2, /device:TPU:0, one launch (start us, length us, event | category | flops | bytes accessed | tf_op | source)
XLA Modules:
  0.0 44.8 jit_solution(15712709908770716581)
XLA Ops:
  0.0 25.1 %exchange.1 = (bf16[4,12,6,768]{3,2,1,0:T(8,128)(2,1)}, bf16[3,3,120,512]{3,2,1,0:T(8,128)(2,1)}, bf16[3,3,512]{2,1,0:T(4,128)(2,1)}, bf16[3,24,512]{2,1,0:T(8,128)(2,1)}) custom-call(bf16[12,6,3072]{2,1,0:T(8,128)(2,1)} %tr_ref.1, bf16[3,120,512]{2,1,0:T(8,128)(2,1)} %bitcast.6, bf16[3,512]{1,0:T(4,128)(2,1)} %te0_ref.1, bf16[24,512]{1,0:T(8,128)(2,1)} %we0_ref.1), custom_call_target="tpu_custom_call" | custom-call | bytes 20971520 | tf_op jit(solution)/shard_map/exchange/pallas_call | solution.py:130
  25.1 19.7 %skin.1 = bf16[36864,128]{1,0:T(8,128)(2,1)} custom-call(bf16[120,768]{1,0:T(8,128)(2,1)} %co_ref.1, bf16[4,12,6,768]{3,2,1,0:T(8,128)(2,1)} %get-tuple-element.9.tr_ref, bf16[3,120,512]{2,1,0:T(8,128)(2,1)} %bitcast.7, bf16[3,512]{1,0:T(4,128)(2,1)} %te0_ref.1, bf16[24,512]{1,0:T(8,128)(2,1)} %we0_ref.1, bf16[3,3,120,512]{3,2,1,0:T(8,128)(2,1)} %get-tuple-element.10.ba_ref, ...), custom_call_target="tpu_custom_call" | custom-call | tf_op jit(solution)/shard_map/skin/pallas_call | solution.py:221

commit v3 on v2

--- a/solution.py
+++ b/solution.py
@@ -40,16 +40,18 @@
     pl.semaphore_wait(barrier, len(partners) + 3)
 
     mine = pl.ds(pl.multiple_of(lax.rem(bat, 2) * half, LANES), half)
-    arrays = ((ba_ref, ba_out), (te_ref, te_out), (we_ref, we_out))
-
-    def hop(slot_from, slot_to, where, send, recv, target):
+    pieces = [((te_ref, te_out), (we_ref, we_out), (ba_ref.at[0], ba_out.at[:, 0]))]
+    pieces += [((ba_ref.at[e], ba_out.at[:, e]),) for e in range(1, ba_ref.shape[0])]
+
+    def hop(slot_from, slot_to, piece, where, send, recv, target):
         made = []
-        for k, (src, dst) in enumerate(arrays):
+        for k, (src, dst) in enumerate(pieces[piece]):
+            at = piece + k if piece == 0 else piece + 2
             lead = (slice(None),) * (len(src.shape) - 1)
             part = src.at[lead + (mine,)] if slot_from == 0 else dst.at[(slot_from - 1,) + lead + (mine,)]
             made.append(pltpu.make_async_remote_copy(
                 src_ref=part, dst_ref=dst.at[(slot_to - 1,) + lead + (mine,)],
-                send_sem=send.at[where, k], recv_sem=recv.at[slot_to - 1, k],
+                send_sem=send.at[where, at], recv_sem=recv.at[slot_to - 1, at],
                 device_id={"blk": target[0], "batch": target[1]},
             ))
         return made
@@ -58,18 +60,44 @@
         for c in copies:
             c.start()
 
-    def arrived(slot):
-        for c in hop(slot, slot, slot - 1, bl_send, bl_recv, (pair, bat)):
+    def first_hop(piece):
+        return hop(0, 2, piece, 1, bl_send, bl_recv, (after, bat))
+
+    def to_odd(piece):
+        return hop(0, 1, piece, 0, bl_send, bl_recv, (pair, bat))
+
+    def odd_forward(piece):
+        return hop(2, 1, piece, 0, bl_send, bl_recv, (pair, bat))
+
+    def even_forward(piece):
+        return hop(2, 3, piece, 2, bl_send, bl_recv, (pair, bat))
+
+    def even_onward(piece):
+        return hop(1, 3, piece, 3, bl_send, bl_recv, (after, bat))
+
+    def share(slot, piece):
+        return hop(slot, slot, piece, slot - 1, fw_send, fw_recv, (blk, sibling))
+
+    def take(slot, piece):
+        for c in hop(slot, slot, piece, slot - 1, bl_send, bl_recv, (pair, bat)):
             c.wait_recv()
-
-    def share(slot):
-        start(hop(slot, slot, slot - 1, fw_send, fw_recv, (blk, sibling)))
-
-    start(hop(0, 2, 1, bl_send, bl_recv, (after, bat)))
-
-    @pl.when(odd == 0)
-    def _():
-        start(hop(0, 1, 0, bl_send, bl_recv, (pair, bat)))
+        if slot == 2:
+            @pl.when(odd == 0)
+            def _():
+                start(even_forward(piece))
+
+            @pl.when(odd == 1)
+            def _():
+                start(odd_forward(piece))
+        if slot == 1:
+            @pl.when(odd == 0)
+            def _():
+                start(even_onward(piece))
+        start(share(slot, piece))
+
+    count = len(pieces)
+    for p in range(count):
+        start(first_hop(p))
 
     moves = []
     for i, q in enumerate(partners):
@@ -80,43 +108,35 @@
             device_id={"blk": blk, "batch": q},
         ))
     start(moves)
+
+    @pl.when(odd == 0)
+    def _():
+        for p in range(count):
+            start(to_odd(p))
+
     own.wait()
     put = pltpu.make_async_copy(stage, tr_out.at[bat], own_sem.at[1])
     put.start()
 
-    arrived(2)
-
-    @pl.when(odd == 0)
-    def _():
-        start(hop(2, 3, 2, bl_send, bl_recv, (pair, bat)))
-
-    @pl.when(odd == 1)
-    def _():
-        start(hop(2, 1, 0, bl_send, bl_recv, (pair, bat)))
-
-    share(2)
-    arrived(1)
-
-    @pl.when(odd == 0)
-    def _():
-        start(hop(1, 3, 3, bl_send, bl_recv, (after, bat)))
-
-    share(1)
-    arrived(3)
-    share(3)
+    for step in range(count + 2):
+        for slot, late in ((2, 0), (1, 1), (3, 2)):
+            if 0 <= step - late < count:
+                take(slot, step - late)
+
     put.wait()
     for c in moves:
         c.wait()
-    for slot in (2, 1, 3):
-        for c in hop(slot, slot, slot - 1, fw_send, fw_recv, (blk, sibling)):
-            c.wait()
-    for c in hop(0, 2, 1, bl_send, bl_recv, (after, bat)) + hop(0, 1, 0, bl_send, bl_recv, (pair, bat)):
-        c.wait_send()
-
-    @pl.when(odd == 0)
-    def _():
-        for c in hop(2, 3, 2, bl_send, bl_recv, (pair, bat)) + hop(1, 3, 3, bl_send, bl_recv, (after, bat)):
+    for p in range(count):
+        for slot in (2, 1, 3):
+            for c in share(slot, p):
+                c.wait()
+        for c in first_hop(p) + to_odd(p):
             c.wait_send()
+
+        @pl.when(odd == 0)
+        def _():
+            for c in even_forward(p) + even_onward(p):
+                c.wait_send()
 
 
 def exchange(n_blk, n_batch, transforms, basis, template, weights):
@@ -140,7 +160,7 @@
         scratch_shapes=[
             pltpu.VMEM((m, jl, chars), BF16),
             dma((n_batch - 1,)), dma((n_batch - 1,)),
-            dma((hop + 1, 3)), dma((hop, 3)), dma((hop, 3)), dma((hop, 3)), dma((2,)),
+            dma((hop + 1, 5)), dma((hop, 5)), dma((hop, 5)), dma((hop, 5)), dma((2,)),
         ],
         compiler_params=pltpu.CompilerParams(
             collective_id=0, has_side_effects=True, vmem_limit_bytes=67043328
@@ -152,7 +172,7 @@
 
 def skin_kernel(
     co_ref, tr_ref, ba0_ref, te0_ref, we0_ref, ba_ref, te_ref, we_ref, out_ref,
-    basis, weights, mixed, poses, coefs,
+    basis, weights, mixed0, mixed1, mixed2, shaped, poses, coefs,
 ):
     rows = co_ref.shape[1]
     k = co_ref.shape[0]
@@ -185,25 +205,28 @@
         parts = [tr_ref[i, m].astype(F32) for i in range(tr_ref.shape[0])]
         poses[m] = jnp.concatenate(parts, axis=0).T.astype(BF16)
 
-    period = 3 * tiles * STEPS
+    group = tiles * STEPS
+    halves = verts // wide
     for s in range(STEPS):
-        for n in range(verts // wide):
-            cols = slice(n * wide, (n + 1) * wide)
-            w = weights[s, :, cols]
-            shaped = [
-                jnp.dot(coefs[...], basis[s, e, :, cols], preferred_element_type=F32)
-                for e in range(3)
-            ]
-            for d in range(3):
+        for n in range(halves):
+            for e in range(3):
+                shaped[s, n, e] = jnp.dot(
+                    coefs[...], basis[s, e, :, n * wide:(n + 1) * wide],
+                    preferred_element_type=F32,
+                )
+    for d, mixed in enumerate((mixed0, mixed1, mixed2)):
+        for s in range(STEPS):
+            for n in range(halves):
+                w = weights[s, :, n * wide:(n + 1) * wide]
                 total = jnp.dot(poses[4 * d + 3], w, preferred_element_type=F32)
                 for e in range(3):
-                    total = total + shaped[e] * jnp.dot(
+                    total = total + shaped[s, n, e] * jnp.dot(
                         poses[4 * d + e], w, preferred_element_type=F32
                     )
                 for h in range(wide // LANES):
-                    at = (d * tiles + n * (wide // LANES) + h) * STEPS + s
-                    mixed[pl.ds(at, rows, stride=period), :] = total[:, h * LANES:(h + 1) * LANES]
-    out_ref[...] = mixed[...].astype(BF16)
+                    at = (n * (wide // LANES) + h) * STEPS + s
+                    mixed[pl.ds(at, rows, stride=group), :] = total[:, h * LANES:(h + 1) * LANES]
+        out_ref[:, d] = mixed[...].reshape(rows, group, LANES).astype(BF16)
 
 
 def skin(coefficients, poses, basis, template, weights, basis_in, template_in, weights_in):
@@ -213,7 +236,7 @@
     joints = weights.shape[0]
     rows = LANES
     depth = -(-(k + 1) // 8) * 8
-    period = 3 * (verts // LANES) * STEPS
+    group = (verts // LANES) * STEPS
 
     def whole(a):
         return pl.BlockSpec(a.shape, lambda i: (0,) * a.ndim)
@@ -221,18 +244,21 @@
     out = pl.pallas_call(
         skin_kernel,
         grid=(chars // rows,),
-        out_shape=jax.ShapeDtypeStruct((chars * period, LANES), BF16),
+        out_shape=jax.ShapeDtypeStruct((chars, 3, group, LANES), BF16),
         in_specs=[
             pl.BlockSpec((k, rows), lambda i: (0, i)),
             pl.BlockSpec((n_batch, comps, jl, rows), lambda i: (0, 0, 0, i)),
             whole(basis), whole(template), whole(weights),
             whole(basis_in), whole(template_in), whole(weights_in),
         ],
-        out_specs=pl.BlockSpec((rows * period, LANES), lambda i: (i, 0)),
+        out_specs=pl.BlockSpec((rows, 3, group, LANES), lambda i: (i, 0, 0, 0)),
         scratch_shapes=[
             pltpu.VMEM((STEPS, 3, depth, verts), BF16),
             pltpu.VMEM((STEPS, joints, verts), BF16),
-            pltpu.VMEM((rows * period, LANES), F32),
+            pltpu.VMEM((rows * group, LANES), F32),
+            pltpu.VMEM((rows * group, LANES), F32),
+            pltpu.VMEM((rows * group, LANES), F32),
+            pltpu.VMEM((STEPS, verts // (2 * LANES), 3, rows, 2 * LANES), F32),
             pltpu.VMEM((comps, rows, joints), BF16),
             pltpu.VMEM((rows, depth), BF16),
         ],

time: 44.9 us -> 42.3 us (0.942)
  Pallas kernels: 44.8 us -> 42.1 us
    pallas_call x1, Pallas kernels: 25.1 us -> 22.5 us  [exchange(): pl.pallas_call(functools.partial(exchange_kernel, n_blk, n_batch), out_sh...]
where the time goes in v3:
time: 42.3 us; the launch traced here: 42.1 us
  Pallas kernels  42.1 us (100%)
    pallas_call x1, Pallas kernels, exchange(): pl.pallas_call(functools.partial(exchange_kernel, n_blk, n_batch), out_sh...  22.5 us
    pallas_call x1, Pallas kernels, skin(): pl.pallas_call(skin_kernel, grid=(chars // rows,), out_shape=jax.ShapeDty...  19.6 us

profile of v3, /device:TPU:0, one launch (start us, length us, event | category | flops | bytes accessed | tf_op | source)
XLA Modules:
  0.0 42.1 jit_solution(9025466826308527941)
XLA Ops:
  0.0 22.5 %exchange.1 = (bf16[4,12,6,768]{3,2,1,0:T(8,128)(2,1)}, bf16[3,3,120,512]{3,2,1,0:T(8,128)(2,1)}, bf16[3,3,512]{2,1,0:T(4,128)(2,1)}, bf16[3,24,512]{2,1,0:T(8,128)(2,1)}) custom-call(bf16[12,6,3072]{2,1,0:T(8,128)(2,1)} %tr_ref.1, bf16[3,120,512]{2,1,0:T(8,128)(2,1)} %bitcast.6, bf16[3,512]{1,0:T(4,128)(2,1)} %te0_ref.1, bf16[24,512]{1,0:T(8,128)(2,1)} %we0_ref.1), custom_call_target="tpu_custom_call" | custom-call | bytes 20971520 | tf_op jit(solution)/shard_map/exchange/pallas_call | solution.py:150
  22.5 19.6 %skin.1 = bf16[768,3,16,128]{3,2,1,0:T(8,128)(2,1)} custom-call(bf16[120,768]{1,0:T(8,128)(2,1)} %co_ref.1, bf16[4,12,6,768]{3,2,1,0:T(8,128)(2,1)} %get-tuple-element.9.tr_ref, bf16[3,120,512]{2,1,0:T(8,128)(2,1)} %bitcast.7, bf16[3,512]{1,0:T(4,128)(2,1)} %te0_ref.1, bf16[24,512]{1,0:T(8,128)(2,1)} %we0_ref.1, ...), custom_call_target="tpu_custom_call" | custom-call | tf_op jit(solution)/shard_map/skin/pallas_call | solution.py:244

commit v4 on v3

--- a/solution.py
+++ b/solution.py
@@ -234,7 +234,7 @@
     n_batch, comps, jl, _ = poses.shape
     verts = weights.shape[1]
     joints = weights.shape[0]
-    rows = LANES
+    rows = 2 * LANES if chars % (2 * LANES) == 0 else LANES
     depth = -(-(k + 1) // 8) * 8
     group = (verts // LANES) * STEPS
 

time: 42.3 us -> 42.3 us (level)
  no operation moved by 1% of the time
where the time goes in v4:
time: 42.3 us; the launch traced here: 42.2 us
  Pallas kernels  42.1 us (100%)
    pallas_call x1, Pallas kernels, exchange(): pl.pallas_call(functools.partial(exchange_kernel, n_blk, n_batch), out_sh...  22.5 us
    pallas_call x1, Pallas kernels, skin(): pl.pallas_call(skin_kernel, grid=(chars // rows,), out_shape=jax.ShapeDty...  19.6 us

profile of v4, /device:TPU:0, one launch (start us, length us, event | category | flops | bytes accessed | tf_op | source)
XLA Modules:
  0.0 42.2 jit_solution(11062369940989269830)
XLA Ops:
  0.0 22.5 %exchange.1 = (bf16[4,12,6,768]{3,2,1,0:T(8,128)(2,1)}, bf16[3,3,120,512]{3,2,1,0:T(8,128)(2,1)}, bf16[3,3,512]{2,1,0:T(4,128)(2,1)}, bf16[3,24,512]{2,1,0:T(8,128)(2,1)}) custom-call(bf16[12,6,3072]{2,1,0:T(8,128)(2,1)} %tr_ref.1, bf16[3,120,512]{2,1,0:T(8,128)(2,1)} %bitcast.6, bf16[3,512]{1,0:T(4,128)(2,1)} %te0_ref.1, bf16[24,512]{1,0:T(8,128)(2,1)} %we0_ref.1), custom_call_target="tpu_custom_call" | custom-call | bytes 20971520 | tf_op jit(solution)/shard_map/exchange/pallas_call | solution.py:150
  22.5 19.6 %skin.1 = bf16[768,3,16,128]{3,2,1,0:T(8,128)(2,1)} custom-call(bf16[120,768]{1,0:T(8,128)(2,1)} %co_ref.1, bf16[4,12,6,768]{3,2,1,0:T(8,128)(2,1)} %get-tuple-element.9.tr_ref, bf16[3,120,512]{2,1,0:T(8,128)(2,1)} %bitcast.7, bf16[3,512]{1,0:T(4,128)(2,1)} %te0_ref.1, bf16[24,512]{1,0:T(8,128)(2,1)} %we0_ref.1, ...), custom_call_target="tpu_custom_call" | custom-call | tf_op jit(solution)/shard_map/skin/pallas_call | solution.py:244
